TPU v7x, 32 devices: a whole 2x2x4 slice. The times are simulated.
32 devices in a mesh: blk: 8 (over z, x), order: 4 (over y, core).
Axes of the slice: x: 2, y: 2, z: 4, core: 2. Of those that a mesh axis runs over, the one named last changes fastest.
Arguments:
- field: float32 [16, 512, 4096], P(None, 'blk', 'order'), may hold values from -6 to 6
- ocean_mask: int32 [512, 4096], P('blk', 'order'), may hold values from 0 to 1, as said below
- plan: int32 [512], replicated, may hold values from 0 to 384, as said below
- legendre: bfloat16 [384, 1024, 1024], P('blk', 'order'), may hold values from -0.4375 to 0.4375
Outputs:
- coefficients: float32 [1024, 16, 2, 1024], P('blk', None, None, 'order')
Inputs may be any that keep to these rules, and one draw needn't show every extreme that they name: `ocean_mask`: exactly 128 cycles are all land, at the ends of the cycle order; every other cycle has an ocean point. plan is 384 exactly at the cycles that are all land, and names every slot below 384 once at the other cycles; slot p belongs to index p // 48 of blk; the cycles of one index of blk name at most 8 slots of one index, and in every draw some index of blk names exactly 8 slots of some index.
All inputs are finite; a program needn't handle non-finite values.
Results may differ from a plain program's by a relative error of at most 0.0029.
Values may be sent and summed in bfloat16 or wider, within the bound.
A program may use at most 128 MiB of HBM per device.

v0:
```python
import math

import jax
import jax.numpy as jnp
from jax import lax
from jax.sharding import PartitionSpec as P

NLON = 4096
M = 1024


def twiddle(first, count):
    longitudes = first + jnp.arange(count, dtype=jnp.int32)
    orders = jnp.arange(M, dtype=jnp.int32)
    product = longitudes[:, None] * orders[None, :] % NLON
    angle = product.astype(jnp.float32) * (2.0 * math.pi / NLON)
    scale = 1.0 / math.sqrt(NLON)
    return jnp.stack([jnp.cos(angle) * scale, -jnp.sin(angle) * scale], axis=1)


def transform(values, table):
    return jnp.einsum("frn,ncm->frcm", values, table, precision=lax.Precision.HIGHEST)


def pack_cycles(masked, plan, slot_dev):
    n_blk = lax.axis_size("blk")
    own_index = lax.axis_index("blk")
    cycle_dev = masked.shape[1]
    cap = (cycle_dev + n_blk - 1) // n_blk
    grid = plan.reshape(n_blk, cycle_dev)
    owner = grid // slot_dev
    positions = jnp.arange(cycle_dev, dtype=jnp.int32)
    earlier = positions[None, :] < positions[:, None]
    same_owner = owner[:, :, None] == owner[:, None, :]
    rank = jnp.sum(same_owner & earlier[None], axis=2, dtype=jnp.int32)
    send_pos = owner * cap + rank
    local_pos = lax.dynamic_index_in_dim(send_pos, own_index, 0, keepdims=False)
    buffer_ids = jnp.arange(n_blk * cap, dtype=jnp.int32)
    send_onehot = (buffer_ids[:, None] == local_pos[None, :]).astype(jnp.float32)
    outgoing = jnp.einsum("qr,frn->fqn", send_onehot, masked, precision=lax.Precision.HIGHEST)
    arrived = lax.all_to_all(outgoing, "blk", split_axis=1, concat_axis=1, tiled=True)
    source_pos = (jnp.arange(n_blk, dtype=jnp.int32)[:, None] * cap + rank).reshape(-1)
    mine = (owner == own_index).reshape(-1)
    slot_local = (grid % slot_dev).reshape(-1)
    slot_ids = jnp.arange(slot_dev, dtype=jnp.int32)
    slot_onehot = ((slot_local[None, :] == slot_ids[:, None]) & mine[None, :]).astype(jnp.float32)
    source_onehot = (source_pos[:, None] == buffer_ids[None, :]).astype(jnp.float32)
    receive_map = jnp.dot(slot_onehot, source_onehot, precision=lax.Precision.HIGHEST)
    return jnp.einsum("pq,fqn->fpn", receive_map, arrived, precision=lax.Precision.HIGHEST)


def degree_sums(legendre, spectrum):
    n_blk = lax.axis_size("blk")
    own_index = lax.axis_index("blk")
    pairs = n_blk // 2
    degree_dev = legendre.shape[2] // n_blk
    own_pair, own_side = own_index // 2, own_index % 2
    swap = [(i, i + 1 - 2 * (i % 2)) for i in range(n_blk)]

    def terms_for(target):
        table = lax.dynamic_slice_in_dim(legendre, target * degree_dev, degree_dev, 2)
        return jnp.einsum("pml,fpcm->lfcm", table, spectrum, preferred_element_type=jnp.float32)

    def pair_sum(step):
        base = (own_pair + step) % pairs * 2
        given = terms_for(base + 1 - own_side).astype(jnp.bfloat16)
        taken = lax.ppermute(given, "blk", swap)
        return terms_for(base + own_side) + taken.astype(jnp.float32)

    steps = sorted(range(1, pairs), key=lambda step: abs(2 * step - pairs))
    arrived = []
    for step in steps:
        shift = [(i, (i + 2 * step) % n_blk) for i in range(n_blk)]
        arrived.append(lax.ppermute(pair_sum(step).astype(jnp.bfloat16), "blk", shift))
    total = pair_sum(0)
    for piece in arrived:
        total = total + piece.astype(jnp.float32)
    return total


def body(field, ocean_mask, plan, legendre):
    lon_local = field.shape[2]
    slot_dev = legendre.shape[0]
    masked = field * ocean_mask.astype(jnp.float32)[None]
    packed = pack_cycles(masked, plan, slot_dev)
    first = lax.axis_index("order") * lon_local
    terms = transform(packed, twiddle(first, lon_local))
    spectrum = lax.psum_scatter(terms, "order", scatter_dimension=3, tiled=True).astype(
        jnp.bfloat16
    )
    coefficients = degree_sums(legendre, spectrum)
    return coefficients


def solution(mesh):
    placed = (P(None, "blk", "order"), P("blk", "order"), P(), P("blk", "order", None))
    return jax.shard_map(
        body, mesh=mesh, in_specs=placed, out_specs=P("blk", None, None, "order"), check_vma=False
    )
```

profile of v0, /device:TPU:8, one launch (start us, length us, event | category | flops | bytes accessed | tf_op | source)
XLA Modules:
  0.0 464.4 jit_solution(10730977180983548286)
XLA Ops:
  7.4 1.0 convert_element_type.80
  8.8 5.5 %fusion.28 = f32[16,64,1024]{2,1,0:T(8,128)S(1)} fusion(f32[16,64,1024]{2,1,0:T(8,128)} %param.4, f32[64,1024]{1,0:T(8,128)S(1)} %convert_element_type.80, s32[64]{0:T(128)S(1)} %fusion.42), kind=kOutput, calls=%fused_computation.46 | convolution fusion | flops 806359040 | bytes 8651008 | tf_op jit(solution)/shard_map/qr,frn->fqn/dot_general | solution.py:40
  14.3 4.5 copy.39
  18.8 6.4 %all-to-all-start = ((f32[16,64,1024]{2,0,1:T(8,128)}), f32[16,64,1024]{2,0,1:T(8,128)}, u32[]{:S(2)}, u32[]{:S(2)}) async-start(f32[16,64,1024]{2,0,1:T(8,128)} %copy.39), calls=%async_computation | async-start | bytes 8388608 | tf_op jit(solution)/shard_map/all_to_all | solution.py:41
  25.6 19.0 %cosine_multiply_fusion = (f32[1024,1,1024]{2,0,1:T(8,128)}, f32[1024,1,1024]{2,0,1:T(8,128)}) fusion(s32[1024]{0:T(1024)S(1)} %iota_add_fusion), kind=kLoop, calls=%fused_computation.23 | loop fusion | flops 17825792 | bytes 8392704 | tf_op jit(solution)/shard_map/mul | solution.py:18
  44.6 71.3 %all-to-all-done = f32[16,64,1024]{2,0,1:T(8,128)} async-done(((f32[16,64,1024]{2,0,1:T(8,128)}), f32[16,64,1024]{2,0,1:T(8,128)}, u32[]{:S(2)}, u32[]{:S(2)}) %all-to-all-start) | async-done | bytes 4194336 | tf_op jit(solution)/shard_map/all_to_all | solution.py:41
  115.9 8.2 %fusion.12 = f32[16,1024,48]{1,2,0:T(8,128)S(1)} fusion(f32[48,64,1]{1,0,2:T(8,128)S(1)} %convolution_bitcast_fusion, f32[16,64,1024]{2,0,1:T(8,128)} %all-to-all-done), kind=kOutput, calls=%fused_computation.20 | convolution fusion | flops 603979776 | bytes 7352320 | tf_op jit(solution)/shard_map/pq,fqn->fpn/dot_general | solution.py:49
  124.1 23.8 %fusion = f32[16,48,2,1024]{3,1,2,0:T(8,128)} fusion(f32[1024,1,1024]{2,0,1:T(8,128)} %get-tuple-element.19, f32[1024,1,1024]{2,0,1:T(8,128)S(1)} %copy-done.7, f32[16,1024,48]{1,2,0:T(8,128)S(1)} %fusion.12), kind=kOutput, calls=%fused_computation.1 | convolution fusion | flops 19329449984 | bytes 17825792 | tf_op jit(solution)/shard_map/frn,ncm->frcm/dot_general | solution.py:22
  148.1 18.5 %constant_dynamic-slice_fusion.6 = (bf16[48,256,128]{2,1,0:T(8,128)(2,1)}, bf16[48,256,128]{2,1,0:T(8,128)(2,1)}, bf16[48,256,128]{2,1,0:T(8,128)(2,1)}, bf16[48...) fusion(bf16[48,256,1024]{2,1,0:T(8,128)(2,1)} %param.7, ...), kind=kLoop, calls=%fused_computation.75 | loop fusion | bytes 50331680 | tf_op jit(solution)/shard_map/dynamic_slice | solution.py:61
  166.6 40.5 %reduce-scatter.2.cloned.1.call-done = f32[16,48,2,256]{3,1,2,0:T(8,128)} async-done(((f32[16,48,2,1024]{3,1,2,0:T(8,128)}), f32[16,48,2,256]{3,1,2,0:T(8,128)}) %reduce-scatter.2.cloned.1.call-update) | async-done | bytes 1572880 | tf_op jit(solution)/shard_map/reduce_scatter | solution.py:88
  207.1 1.5 convert_element_type.83
  208.6 3.2 copy.42
  211.9 4.0 convert_bitcast_fusion
  215.9 1.5 collective-permute-start.5
  217.4 2.0 convert_bitcast_fusion.2
  220.1 2.0 convert_bitcast_fusion.1
  222.1 1.5 collective-permute-start.3
  223.6 2.0 convert_bitcast_fusion.3
  226.2 38.2 %collective-permute-done.5 = bf16[128,16,2,256]{0,1,2,3:T(8,128)(2,1)S(1)} collective-permute-done((bf16[128,16,2,256]{0,1,2,3:T(8,128)(2,1)S(1)}, bf16[128,16,2,256]{0,1,2,3:T(8,128)(2,1)S(1)}, u32[]{:S(2)}, u32[]{:S(2)}) %collective-permute-start.5) | collective-permute-done | bytes 2097184 | tf_op jit(solution)/shard_map/ppermute | solution.py:67
  264.5 2.5 fusion.6
  267.8 41.6 %collective-permute-done.1 = bf16[128,16,2,256]{0,1,2,3:T(8,128)(2,1)S(1)} collective-permute-done((bf16[128,16,2,256]{0,1,2,3:T(8,128)(2,1)S(1)}, bf16[128,16,2,256]{0,1,2,3:T(8,128)(2,1)S(1)}, u32[]{:S(2)}, u32[]{:S(2)}) %collective-permute-start.1) | collective-permute-done | bytes 2097184 | tf_op jit(solution)/shard_map/ppermute | solution.py:67
  309.4 2.5 fusion.8
  311.9 2.5 collective-permute-start.2
  314.4 40.0 %collective-permute-done.3 = bf16[128,16,2,256]{0,1,2,3:T(8,128)(2,1)S(1)} collective-permute-done((bf16[128,16,2,256]{0,1,2,3:T(8,128)(2,1)S(1)}, bf16[128,16,2,256]{0,1,2,3:T(8,128)(2,1)S(1)}, u32[]{:S(2)}, u32[]{:S(2)}) %collective-permute-start.3) | collective-permute-done | bytes 2097184 | tf_op jit(solution)/shard_map/ppermute | solution.py:67
  354.4 2.5 fusion.7
  356.9 1.5 collective-permute-start.4
  358.4 2.1 fusion.26
  360.4 37.6 %collective-permute-done = bf16[128,16,2,256]{0,1,2,3:T(8,128)(2,1)S(1)} collective-permute-done((bf16[128,16,2,256]{0,1,2,3:T(8,128)(2,1)S(1)}, bf16[128,16,2,256]{0,1,2,3:T(8,128)(2,1)S(1)}, u32[]{:S(2)}, u32[]{:S(2)}) %collective-permute-start) | collective-permute-done | bytes 2097184 | tf_op jit(solution)/shard_map/ppermute | solution.py:67
  398.0 5.1 %collective-permute-done.2 = bf16[128,16,2,256]{0,1,2,3:T(8,128)(2,1)S(1)} collective-permute-done((bf16[128,16,2,256]{0,1,2,3:T(8,128)(2,1)S(1)}, bf16[128,16,2,256]{0,1,2,3:T(8,128)(2,1)S(1)}, u32[]{:S(2)}, u32[]{:S(2)}) %collective-permute-start.2) | collective-permute-done | bytes 2097184 | tf_op jit(solution)/shard_map/ppermute | solution.py:74
  403.1 44.8 %collective-permute-done.4 = bf16[128,16,2,256]{0,1,2,3:T(8,128)(2,1)S(1)} collective-permute-done((bf16[128,16,2,256]{0,1,2,3:T(8,128)(2,1)S(1)}, bf16[128,16,2,256]{0,1,2,3:T(8,128)(2,1)S(1)}, u32[]{:S(2)}, u32[]{:S(2)}) %collective-permute-start.4) | collective-permute-done | bytes 2097184 | tf_op jit(solution)/shard_map/ppermute | solution.py:74
  448.0 3.4 fusion.11
  451.3 5.8 %copy.57 = f32[128,16,2,256]{3,2,1,0:T(2,128)} copy(f32[128,16,2,256]{0,1,2,3:T(8,128)} %fusion.11) | data formatting | bytes 8388608 | tf_op jit(solution)/shard_map/add | solution.py:77
  (37 shorter events, 3.8 us)
Async XLA Ops:
  18.8 6.5 %copy-start.8 = (s32[512]{0:T(512)S(1)}, s32[512]{0:T(512)}, u32[]{:S(2)}) copy-start(s32[512]{0:T(512)} %param.6) | copy-start | bytes 6148
  18.8 97.1 %all-to-all-start = ((f32[16,64,1024]{2,0,1:T(8,128)}), f32[16,64,1024]{2,0,1:T(8,128)}, u32[]{:S(2)}, u32[]{:S(2)}) async-start(f32[16,64,1024]{2,0,1:T(8,128)} %copy.39), calls=%async_computation | async-start | bytes 8388608 | tf_op jit(solution)/shard_map/all_to_all | solution.py:41
  25.2 181.9 %reduce-scatter.2.cloned.1.call-start = ((), (), s32[]{:S(2)}) async-start(), calls=%async_computation.2 | async-start | bytes 7864320 | tf_op jit(solution)/shard_map/reduce_scatter | solution.py:88
  115.9 8.2 %copy-start.7 = (f32[1024,1,1024]{2,0,1:T(8,128)S(1)}, f32[1024,1,1024]{2,0,1:T(8,128)}, u32[]{:S(2)}) copy-start(f32[1024,1,1024]{2,0,1:T(8,128)} %get-tuple-element.18) | copy-start | bytes 12582916
  211.9 5.6 %copy-start.2 = (bf16[48,256,128]{2,1,0:T(8,128)(2,1)S(1)}, bf16[48,256,128]{2,1,0:T(8,128)(2,1)}, u32[]{:S(2)}) copy-start(bf16[48,256,128]{2,1,0:T(8,128)(2,1)} %get-tuple-element.12) | copy-start | bytes 9437188
  215.9 48.6 %collective-permute-start.5 = (bf16[128,16,2,256]{0,1,2,3:T(8,128)(2,1)S(1)}, bf16[128,16,2,256]{0,1,2,3:T(8,128)(2,1)S(1)}, u32[]{:S(2)}, u32[]{:S(2)}) collective-permute-start(bf16[128,16,2,256]{0,1,2,3:T(8,128)(2,1)S(1)} %convert_bitcast_fusion), channel_id=1, source_target_pairs={{0,4},{4,0},{8,12},{12,8},{16,20},{20,16},{24,28},{28,24},{1,5},{5... | collective-permute-start | bytes 6291464 | tf_op jit(solution)/shard_map/ppermute | solution.py:67
  217.4 2.6 copy-start.1
  219.4 90.0 %collective-permute-start.1 = (bf16[128,16,2,256]{0,1,2,3:T(8,128)(2,1)S(1)}, bf16[128,16,2,256]{0,1,2,3:T(8,128)(2,1)S(1)}, u32[]{:S(2)}, u32[]{:S(2)}) collective-permute-start(bf16[128,16,2,256]{0,1,2,3:T(8,128)(2,1)S(1)} %convert_bitcast_fusion.2), channel_id=1, source_target_pairs={{0,4},{4,0},{8,12},{12,8},{16,20},{20,16},{24,28},{28,24},{1,5},{5... | collective-permute-start | bytes 6291464 | tf_op jit(solution)/shard_map/ppermute | solution.py:67
  220.1 3.5 copy-start
  222.1 132.3 %collective-permute-start.3 = (bf16[128,16,2,256]{0,1,2,3:T(8,128)(2,1)S(1)}, bf16[128,16,2,256]{0,1,2,3:T(8,128)(2,1)S(1)}, u32[]{:S(2)}, u32[]{:S(2)}) collective-permute-start(bf16[128,16,2,256]{0,1,2,3:T(8,128)(2,1)S(1)} %convert_bitcast_fusion.1), channel_id=1, source_target_pairs={{0,4},{4,0},{8,12},{12,8},{16,20},{20,16},{24,28},{28,24},{1,5},{5... | collective-permute-start | bytes 6291464 | tf_op jit(solution)/shard_map/ppermute | solution.py:67
  223.6 40.9 %copy-start.6 = (bf16[48,256,128]{2,1,0:T(8,128)(2,1)S(1)}, bf16[48,256,128]{2,1,0:T(8,128)(2,1)}, u32[]{:S(2)}) copy-start(bf16[48,256,128]{2,1,0:T(8,128)(2,1)} %get-tuple-element.9) | copy-start | bytes 9437188
  225.6 172.4 %collective-permute-start = (bf16[128,16,2,256]{0,1,2,3:T(8,128)(2,1)S(1)}, bf16[128,16,2,256]{0,1,2,3:T(8,128)(2,1)S(1)}, u32[]{:S(2)}, u32[]{:S(2)}) collective-permute-start(bf16[128,16,2,256]{0,1,2,3:T(8,128)(2,1)S(1)} %convert_bitcast_fusion.3), channel_id=1, source_target_pairs={{0,4},{4,0},{8,12},{12,8},{16,20},{20,16},{24,28},{28,24},{1,5},{5... | collective-permute-start | bytes 6291464 | tf_op jit(solution)/shard_map/ppermute | solution.py:67
  264.5 44.9 %copy-start.5 = (bf16[48,256,128]{2,1,0:T(8,128)(2,1)S(1)}, bf16[48,256,128]{2,1,0:T(8,128)(2,1)}, u32[]{:S(2)}) copy-start(bf16[48,256,128]{2,1,0:T(8,128)(2,1)} %get-tuple-element.13) | copy-start | bytes 9437188
  267.0 131.0 %collective-permute-start.6 = (bf16[128,16,2,256]{0,1,2,3:T(8,128)(2,1)S(1)}, bf16[128,16,2,256]{0,1,2,3:T(8,128)(2,1)S(1)}, u32[]{:S(2)}, u32[]{:S(2)}) collective-permute-start(bf16[128,16,2,256]{0,1,2,3:T(8,128)(2,1)S(1)} %fusion.6), channel_id=1, source_target_pairs={{0,24},{4,28},{8,0},{12,4},{16,8},{20,12},{24,16},{28,20},{1,25},{... | collective-permute-start | bytes 6291464 | tf_op jit(solution)/shard_map/ppermute | solution.py:74
  309.4 44.9 %copy-start.4 = (bf16[48,256,128]{2,1,0:T(8,128)(2,1)S(1)}, bf16[48,256,128]{2,1,0:T(8,128)(2,1)}, u32[]{:S(2)}) copy-start(bf16[48,256,128]{2,1,0:T(8,128)(2,1)} %get-tuple-element.11) | copy-start | bytes 9437188
  311.9 91.2 %collective-permute-start.2 = (bf16[128,16,2,256]{0,1,2,3:T(8,128)(2,1)S(1)}, bf16[128,16,2,256]{0,1,2,3:T(8,128)(2,1)S(1)}, u32[]{:S(2)}, u32[]{:S(2)}) collective-permute-start(bf16[128,16,2,256]{0,1,2,3:T(8,128)(2,1)S(1)} %fusion.8), channel_id=1, source_target_pairs={{0,16},{4,20},{8,24},{12,28},{16,0},{20,4},{24,8},{28,12},{1,17},{... | collective-permute-start | bytes 6291464 | tf_op jit(solution)/shard_map/ppermute | solution.py:74
  354.4 4.0 copy-start.3
  356.9 91.1 %collective-permute-start.4 = (bf16[128,16,2,256]{0,1,2,3:T(8,128)(2,1)S(1)}, bf16[128,16,2,256]{0,1,2,3:T(8,128)(2,1)S(1)}, u32[]{:S(2)}, u32[]{:S(2)}) collective-permute-start(bf16[128,16,2,256]{0,1,2,3:T(8,128)(2,1)S(1)} %fusion.7), channel_id=1, source_target_pairs={{0,8},{4,12},{8,16},{12,20},{16,24},{20,28},{24,0},{28,4},{1,9},{5... | collective-permute-start | bytes 6291464 | tf_op jit(solution)/shard_map/ppermute | solution.py:74
Sparse Core Ops, SparseCore 0:
  148.1 58.9 reduce-scatter.1
where the time goes:
time: 474 us; the launch traced here: 464 us
  waiting for transfers between devices  319 us (67%)
  matrix products  57.3 us (12%)
  local copies, waits for them, and re-layouts  32.3 us (7%)
  other arithmetic  26 us (5%)
  starting transfers between devices  15.5 us (3%)
  between operations  14.1 us (3%)
    ppermute x4, waiting for transfers between devices, pair_sum(): taken = lax.ppermute(given, 'blk', swap)  157 us
    all_to_all x1, waiting for transfers between devices, pack_cycles(): lax.all_to_all(outgoing, 'blk', split_axis=1, concat_axis=1, tiled=True)  71.3 us
    ppermute x3, waiting for transfers between devices, degree_sums(): lax.ppermute(pair_sum(step).astype(jnp.bfloat16), 'blk', shift)  50 us
    reduce_scatter x1, waiting for transfers between devices, body(): lax.psum_scatter(terms, 'order', scatter_dimension=3, tiled=True)  40.5 us
    dot_general x1, matrix products, transform(): jnp.einsum('frn,ncm->frcm', values, table, precision=lax.Precision.HIGHEST)  23.8 us
    dot_general x8, matrix products, terms_for(): jnp.einsum('pml,fpcm->lfcm', table, spectrum, preferred_element_type=jnp....  19.6 us
    mul x1, other arithmetic, twiddle(): return jnp.stack([jnp.cos(angle) * scale, -jnp.sin(angle) * scale], axis=1)  19 us
    dynamic_slice x1, local copies, waits for them, and re-layouts, terms_for(): lax.dynamic_slice_in_dim(legendre, target * degree_dev, degree_dev, 2)  18.5 us
  transfers between devices with their start and end apart: 9, of which 8 were waited for; matrix products, arithmetic and copies ran while one was open for 12% of the time, Pallas kernels for 0%

commit v1 on v0

--- a/solution.py
+++ b/solution.py
@@ -1,12 +1,494 @@
+import functools
 import math
 
 import jax
 import jax.numpy as jnp
+import numpy as np
 from jax import lax
+from jax.experimental import pallas as pl
+from jax.experimental.pallas import tpu as pltpu
 from jax.sharding import PartitionSpec as P
 
 NLON = 4096
 M = 1024
+MESH = pl.DeviceIdType.MESH
+F32, BF16 = jnp.float32, jnp.bfloat16
+
+LINE, PAIR = 4, 2
+CHUNK = 2
+BASE = 32
+
+
+def table_of(lon_local, orders):
+    coarse = np.arange(lon_local // BASE)[:, None] * BASE
+    fine = np.arange(BASE)[:, None]
+    m = np.arange(M)[None, :]
+
+    def parts(n, scale):
+        angle = (n * m % NLON) * (2.0 * math.pi / NLON)
+        return [np.cos(angle) * scale, np.sin(angle) * scale]
+
+    both = parts(coarse, 1.0) + parts(fine, 1.0 / math.sqrt(NLON))
+    owners = M // orders
+    stacked = np.stack([t.reshape(BASE, owners, orders) for t in both])
+    return stacked.transpose(2, 0, 1, 3).astype(np.float32)
+
+
+def plan_maps(plan, cycle_dev, slot_dev, orders_tile):
+    n_blk = lax.axis_size("blk")
+    own_index = lax.axis_index("blk")
+    cap = (cycle_dev + n_blk - 1) // n_blk
+    grid = plan.reshape(n_blk, cycle_dev)
+    owner = grid // slot_dev
+    positions = jnp.arange(cycle_dev, dtype=jnp.int32)
+    earlier = positions[None, :] < positions[:, None]
+    same_owner = owner[:, :, None] == owner[:, None, :]
+    rank = jnp.sum(same_owner & earlier[None], axis=2, dtype=jnp.int32)
+    send_pos = owner * cap + rank
+    local_pos = lax.dynamic_index_in_dim(send_pos, own_index, 0, keepdims=False)
+    source_pos = (jnp.arange(n_blk, dtype=jnp.int32)[:, None] * cap + rank).reshape(-1)
+    lanes = jnp.arange(slot_dev * orders_tile, dtype=jnp.int32) // orders_tile
+    wanted = own_index * slot_dev + lanes
+    hit = plan.reshape(-1)[:, None] == wanted[None, :]
+    received = jnp.sum(jnp.where(hit, source_pos[:, None], 0), axis=0, dtype=jnp.int32)
+    return jnp.tile(local_pos, CHUNK)[None, :], received[None, :]
+
+
+def fused_kernel(
+    dims,
+    field, mask, legendre, table, send_lanes, recv_lanes,
+    out, far_field,
+    leg, spread, own_part, xs, xr, zr, wh, wl, near, far, mask_near, mask_far, parts,
+    y_own, y_send, y_recv, a_send, a_recv, pick, pack, stage, tabs,
+    leg_sem, near_sem, far_sem, mask_sem, tab_sem, out_sem,
+    pf_send, pf_recv, pm_send, pm_recv, ys_sem, yr_sem, as_sem, ar_sem,
+    xs_sem, xr_sem, zs_sem, zr_sem,
+):
+    n, groups, tile, m_dev, l_dev, cyc, lon, slot_dev, cap = dims
+    rows = CHUNK * cyc
+    n_blk = LINE * PAIR
+    b = lax.axis_index("blk")
+    o = lax.axis_index("order")
+    z, x = b // PAIR, b % PAIR
+    side = z // 2
+    odd = z % 2
+    is_end = 1 - (odd + side - 2 * odd * side)
+    far_end = (LINE - 1) * (1 - side)
+    far_inner = 2 - side
+    mate = 2 * side + 1 - odd
+    dest = [
+        is_end * far_end + (1 - is_end) * mate,
+        is_end * far_inner + (1 - is_end) * far_end,
+        is_end * mate + (1 - is_end) * far_inner,
+        z,
+    ]
+    x_peer = b + 1 - 2 * x
+    y_peer = (o + 2) % 4
+    c_peer = o + 1 - 2 * (o % 2)
+
+    def remote(src, dst, send, recv, blk, order):
+        return pltpu.make_async_remote_copy(
+            src_ref=src, dst_ref=dst, send_sem=send, recv_sem=recv,
+            device_id=(blk, order), device_id_type=MESH,
+        )
+
+    def leg_copy(half, j):
+        block = dest[j] * PAIR + (x if half == 0 else 1 - x)
+        lanes = pl.ds(pl.multiple_of(block * l_dev, l_dev), l_dev)
+        return pltpu.make_async_copy(
+            legendre.at[:, :, lanes],
+            leg.at[half, :, :, pl.ds(j * l_dev, l_dev)],
+            leg_sem.at[half, j],
+        )
+
+    def near_copy(h):
+        return pltpu.make_async_copy(
+            field.at[pl.ds(h * CHUNK, CHUNK)], near.at[h % 2], near_sem.at[h % 2]
+        )
+
+    def far_copy(h):
+        return pltpu.make_async_copy(
+            far_field.at[pl.ds(h * CHUNK, CHUNK)], far.at[h % 2], far_sem.at[h % 2]
+        )
+
+    def push_field(h):
+        fields = pl.ds(h * CHUNK, CHUNK)
+        return remote(
+            field.at[fields], far_field.at[fields], pf_send.at[h], pf_recv.at[h], b, c_peer
+        )
+
+    tab_own = pltpu.make_async_copy(table.at[o], tabs.at[0], tab_sem.at[0])
+    tab_other = pltpu.make_async_copy(table.at[y_peer], tabs.at[1], tab_sem.at[1])
+    tab_own.start()
+    tab_other.start()
+    mask_own = pltpu.make_async_copy(mask, mask_near, mask_sem)
+    mask_own.start()
+    near_copy(0).start()
+
+    barrier = pltpu.get_barrier_semaphore()
+    for k in range(1, n_blk):
+        pl.semaphore_signal(barrier, inc=1, device_id=((b + k) % n_blk, o), device_id_type=MESH)
+    pl.semaphore_signal(barrier, inc=1, device_id=(b, y_peer), device_id_type=MESH)
+    pl.semaphore_signal(barrier, inc=1, device_id=(b, c_peer), device_id_type=MESH)
+    pl.semaphore_wait(barrier, n_blk + 1)
+
+    push_mask = remote(mask, mask_far, pm_send, pm_recv, b, c_peer)
+    push_mask.start()
+
+    @pl.loop(0, n)
+    def _(h):
+        push_field(h).start()
+
+    for half in (1, 0):
+        for j in range(LINE):
+            leg_copy(half, j).start()
+
+    def iota(shape, axis):
+        return lax.broadcasted_iota(jnp.int32, shape, axis)
+
+    r = iota((rows, rows), 0)
+    lane = iota((rows, rows), 1)
+    per = CHUNK * cap
+    position = r // per * cap + r % cap
+    hit = (position == send_lanes[...]) & (r % per // cap == lane // cyc)
+    pack[...] = jnp.where(hit, 1.0, 0.0).astype(BF16)
+    r = iota((rows, slot_dev * tile), 0)
+    position = r // per * cap + r % cap
+    for f in range(CHUNK):
+        hit = (position == recv_lanes[...]) & (r % per // cap == f)
+        pick[f] = jnp.where(hit, 1.0, 0.0).astype(BF16)
+
+    tab_own.wait()
+    tab_other.wait()
+    for side_of in range(2):
+
+        @pl.loop(0, lon // BASE)
+        def _(a):
+            ca = tabs[side_of, 0, pl.ds(a, 1), :]
+            sa = tabs[side_of, 1, pl.ds(a, 1), :]
+            cb = tabs[side_of, 2]
+            sb = tabs[side_of, 3]
+            at = pl.ds(pl.multiple_of(a * BASE, BASE), BASE)
+            for c, value in enumerate((ca * cb - sa * sb, -(sa * cb + ca * sb))):
+                high = value.astype(BF16)
+                wh[side_of, at, pl.ds(c * m_dev, m_dev)] = high
+                rest = value - high.astype(F32)
+                wl[side_of, at, pl.ds(c * m_dev, m_dev)] = rest.astype(BF16)
+
+    mask_own.wait()
+    push_mask.wait_recv()
+    push_field(0).wait_recv()
+    far_copy(0).start()
+
+    def turn(index):
+        quarter = (index * iota((1, m_dev), 1)) % 4
+        real = jnp.where(quarter == 0, 1.0, jnp.where(quarter == 2, -1.0, 0.0))
+        imag = jnp.where(quarter == 3, 1.0, jnp.where(quarter == 1, -1.0, 0.0))
+        return real, imag
+
+    def y_copy(h):
+        return remote(y_send.at[h % 2], y_recv.at[h], ys_sem.at[h % 2], yr_sem.at[h], b, y_peer)
+
+    def transform(h):
+        near_copy(h).wait()
+        far_copy(h).wait()
+
+        @pl.when(h + 1 < n)
+        def _():
+            near_copy(h + 1).start()
+            push_field(h + 1).wait_recv()
+            far_copy(h + 1).start()
+
+        @pl.when(h >= 2)
+        def _():
+            y_copy(h - 2).wait_send()
+
+        for i, (data, wet) in enumerate(((near, mask_near), (far, mask_far))):
+            value = (data[h % 2] * wet[...].astype(F32)[None]).reshape(rows, lon)
+            high = value.astype(BF16)
+            parts[pl.ds(i * rows, rows), :] = high
+            rest = value - high.astype(F32)
+            parts[pl.ds((2 + i) * rows, rows), :] = rest.astype(BF16)
+        near_r, near_i = turn(o)
+        far_r, far_i = turn(c_peer)
+        for side_of in (1, 0):
+            both = jnp.dot(parts[...], wh[side_of], preferred_element_type=F32)
+            total = both[: 2 * rows] + both[2 * rows :]
+            total += jnp.dot(
+                parts[pl.ds(0, 2 * rows), :], wl[side_of], preferred_element_type=F32
+            )
+            nr, ni = total[:rows, :m_dev], total[:rows, m_dev:]
+            fr, fi = total[rows:, :m_dev], total[rows:, m_dev:]
+            real = near_r * nr - near_i * ni + far_r * fr - far_i * fi
+            imag = near_r * ni + near_i * nr + far_r * fi + far_i * fr
+            target = y_send if side_of else y_own
+            target[h % 2, :, pl.ds(0, m_dev)] = real
+            target[h % 2, :, pl.ds(m_dev, m_dev)] = imag
+            if side_of:
+                y_copy(h).start()
+
+    def a_copy(h, k):
+        to = (b + k) % n_blk
+        return remote(
+            a_send.at[h, to], a_recv.at[h, b], as_sem.at[h, k - 1], ar_sem.at[h, k - 1], to, o
+        )
+
+    def exchange(h):
+        y_copy(h).wait_recv()
+        spectrum = (y_own[h % 2] + y_recv[h]).astype(BF16)
+        packed = jnp.dot(pack[...], spectrum, preferred_element_type=F32).astype(BF16)
+        a_send[h] = packed.reshape(n_blk, per, 2 * m_dev)
+        a_recv[h, b] = a_send[h, b]
+        for k in range(1, n_blk):
+            a_copy(h, k).start()
+
+    diagonal = (iota((1, tile, slot_dev * tile), 1)) == (iota((1, tile, slot_dev * tile), 2) % tile)
+
+    def spread_out(h):
+        for k in range(1, n_blk):
+            a_copy(h, k).wait_recv()
+        got = a_recv[h].reshape(rows, 2 * m_dev)
+        for c in range(2):
+            for f in range(CHUNK):
+                value = lax.dot_general(
+                    got[:, c * m_dev : (c + 1) * m_dev], pick[f],
+                    (((0,), (0,)), ((), ())), preferred_element_type=F32,
+                )
+                value = value.reshape(groups, tile, slot_dev * tile)
+                spread[:, pl.ds((f * 2 + c) * tile, tile), :] = jnp.where(
+                    diagonal, value, 0.0
+                ).astype(BF16)
+
+    def x_copy(h, j):
+        return remote(
+            xs.at[h % 2, j], xr.at[h % 5, j], xs_sem.at[h % 2, j], xr_sem.at[h, j], x_peer, o
+        )
+
+    def product(g, half):
+        at = pl.ds(pl.multiple_of(g * tile, tile), tile)
+        table_part = leg[half, :, at, :].reshape(slot_dev * tile, LINE * l_dev)
+        return at, jnp.dot(spread[g], table_part, preferred_element_type=F32)
+
+    def products(h):
+        @pl.when(h == 0)
+        def _():
+            for j in range(LINE):
+                leg_copy(1, j).wait()
+
+        @pl.when(h >= 2)
+        def _():
+            for j in range(LINE):
+                x_copy(h - 2, j).wait_send()
+
+        @pl.loop(0, groups)
+        def _(g):
+            at, value = product(g, 1)
+            for j in range(LINE):
+                piece = value[:, j * l_dev : (j + 1) * l_dev].reshape(2 * CHUNK, tile, l_dev)
+                xs[h % 2, j, :, at, :] = piece.astype(BF16)
+
+        for j in range(LINE):
+            x_copy(h, j).start()
+
+        @pl.when(h == 0)
+        def _():
+            for j in range(LINE):
+                leg_copy(0, j).wait()
+
+        @pl.loop(0, groups)
+        def _(g):
+            at, value = product(g, 0)
+            for j in range(LINE):
+                piece = value[:, j * l_dev : (j + 1) * l_dev].reshape(2 * CHUNK, tile, l_dev)
+                own_part[h % 3, j, :, at, :] = piece
+
+    def z_copy(h, j, to_z, slot):
+        return remote(
+            xr.at[h % 5, j], zr.at[h % 4, slot], zs_sem.at[h, j], zr_sem.at[h, slot],
+            to_z * PAIR + x, o,
+        )
+
+    def end_copy(h, j):
+        return z_copy(h, j, mate, j)
+
+    def inner_copy(h, j):
+        return z_copy(h, j, (mate, far_end, far_inner)[j], (0, 1, 3)[j])
+
+    def first_sums(h):
+        for j in range(LINE):
+            x_copy(h, j).wait_recv()
+            value = own_part[h % 3, j] + xr[h % 5, j].astype(F32)
+            if j == LINE - 1:
+                own_part[h % 3, j] = value
+                continue
+
+            @pl.when(is_end == 1)
+            def _():
+                xr[h % 5, j] = value.astype(BF16)
+                end_copy(h, j).start()
+
+            @pl.when(is_end == 0)
+            def _():
+                if j == 0:
+                    xr[h % 5, j] = value.astype(BF16)
+                    inner_copy(h, j).start()
+                else:
+                    own_part[h % 3, j] = value
+
+    def second_sums(h):
+        @pl.when(is_end == 0)
+        def _():
+            for j in (1, 2):
+                end_copy(h, j - 1).wait_recv()
+                value = own_part[h % 3, j] + zr[h % 4, j - 1].astype(F32)
+                xr[h % 5, j] = value.astype(BF16)
+                inner_copy(h, j).start()
+
+    def out_copy(h):
+        return pltpu.make_async_copy(stage.at[h % 2], out.at[h], out_sem.at[h % 2])
+
+    def last_sums(h):
+        @pl.when(h >= 2)
+        def _():
+            out_copy(h - 2).wait()
+
+        @pl.when(is_end == 1)
+        def _():
+            inner_copy(h, 0).wait_recv()
+            inner_copy(h, 1).wait_recv()
+            stage[h % 2] = own_part[h % 3, 3] + zr[h % 4, 0].astype(F32) + zr[h % 4, 1].astype(F32)
+            for j in range(3):
+                end_copy(h, j).wait_send()
+
+        @pl.when(is_end == 0)
+        def _():
+            end_copy(h, 2).wait_recv()
+            inner_copy(h, 2).wait_recv()
+            stage[h % 2] = own_part[h % 3, 3] + zr[h % 4, 2].astype(F32) + zr[h % 4, 3].astype(F32)
+            for j in range(3):
+                inner_copy(h, j).wait_send()
+
+        out_copy(h).start()
+
+    @pl.loop(0, n + 5)
+    def _(t):
+        def when(step, delay):
+            @pl.when((t >= delay) & (t < n + delay))
+            def _():
+                step(t - delay)
+
+        when(last_sums, 5)
+        when(transform, 0)
+        when(exchange, 1)
+        when(spread_out, 2)
+        when(products, 2)
+        when(second_sums, 4)
+        when(first_sums, 3)
+
+    push_mask.wait_send()
+
+    @pl.loop(0, n)
+    def _(h):
+        push_field(h).wait_send()
+        for k in range(1, n_blk):
+            a_copy(h, k).wait_send()
+
+    for h in (n - 2, n - 1):
+        y_copy(h).wait_send()
+        out_copy(h).wait()
+        for j in range(LINE):
+            x_copy(h, j).wait_send()
+
+
+def fused_body(field, ocean_mask, plan, legendre):
+    fields, cyc, lon = field.shape
+    slot_dev, m_dev, degrees = legendre.shape
+    n_blk = LINE * PAIR
+    l_dev = degrees // n_blk
+    tile = 16
+    groups = m_dev // tile
+    n = fields // CHUNK
+    rows = CHUNK * cyc
+    cap = (cyc + n_blk - 1) // n_blk
+    per = CHUNK * cap
+    send_lanes, recv_lanes = plan_maps(plan, cyc, slot_dev, tile)
+    table = jnp.asarray(table_of(lon, m_dev))
+    piece = (2 * CHUNK, m_dev, l_dev)
+    dma = pltpu.SemaphoreType.DMA
+    any_spec = pl.BlockSpec(memory_space=pl.ANY)
+    vmem_spec = pl.BlockSpec(memory_space=pltpu.VMEM)
+    scratch = [
+        pltpu.VMEM((2, slot_dev, m_dev, LINE * l_dev), BF16),
+        pltpu.VMEM((groups, 2 * CHUNK * tile, slot_dev * tile), BF16),
+        pltpu.VMEM((3, LINE) + piece, F32),
+        pltpu.VMEM((2, LINE) + piece, BF16),
+        pltpu.VMEM((5, LINE) + piece, BF16),
+        pltpu.VMEM((4, 4) + piece, BF16),
+        pltpu.VMEM((2, lon, 2 * m_dev), BF16),
+        pltpu.VMEM((2, lon, 2 * m_dev), BF16),
+        pltpu.VMEM((2, CHUNK, cyc, lon), F32),
+        pltpu.VMEM((2, CHUNK, cyc, lon), F32),
+        pltpu.VMEM((cyc, lon), jnp.int32),
+        pltpu.VMEM((cyc, lon), jnp.int32),
+        pltpu.VMEM((4 * rows, lon), BF16),
+        pltpu.VMEM((2, rows, 2 * m_dev), F32),
+        pltpu.VMEM((2, rows, 2 * m_dev), F32),
+        pltpu.VMEM((n, rows, 2 * m_dev), F32),
+        pltpu.VMEM((n, n_blk, per, 2 * m_dev), BF16),
+        pltpu.VMEM((n, n_blk, per, 2 * m_dev), BF16),
+        pltpu.VMEM((CHUNK, rows, slot_dev * tile), BF16),
+        pltpu.VMEM((rows, rows), BF16),
+        pltpu.VMEM((2,) + piece, F32),
+        pltpu.VMEM((2, 4, BASE, m_dev), F32),
+        dma((2, LINE)),
+        dma((2,)),
+        dma((2,)),
+        dma,
+        dma((2,)),
+        dma((2,)),
+        dma((n,)), dma((n,)),
+        dma, dma,
+        dma((2,)), dma((n,)),
+        dma((n, n_blk - 1)), dma((n, n_blk - 1)),
+        dma((2, LINE)), dma((n, LINE)),
+        dma((n, 3)), dma((n, 4)),
+    ]
+    dims = (n, groups, tile, m_dev, l_dev, cyc, lon, slot_dev, cap)
+    sums, _ = pl.pallas_call(
+        functools.partial(fused_kernel, dims),
+        out_shape=[
+            jax.ShapeDtypeStruct((n,) + piece, F32),
+            jax.ShapeDtypeStruct(field.shape, F32),
+        ],
+        in_specs=[any_spec] * 4 + [vmem_spec] * 2,
+        out_specs=[any_spec] * 2,
+        scratch_shapes=scratch,
+        compiler_params=pltpu.CompilerParams(
+            collective_id=0, has_side_effects=True, vmem_limit_bytes=66 * 1000 * 1000
+        ),
+        name="analysis",
+    )(field, ocean_mask, legendre, table, send_lanes, recv_lanes)
+    sums = sums.reshape(fields, 2, m_dev, l_dev)
+    return jnp.transpose(sums, (3, 0, 1, 2))
+
+
+def fits(mesh, field, legendre):
+    shape = dict(mesh.shape)
+    n_blk, n_order = shape["blk"], shape["order"]
+    cyc, lon = field.shape[1] // n_blk, field.shape[2] // n_order
+    slots, m_dev = legendre.shape[0] // n_blk, legendre.shape[1] // n_order
+    return (
+        n_blk == LINE * PAIR
+        and n_order == 4
+        and field.shape[0] % CHUNK == 0
+        and field.shape[0] // CHUNK >= 5
+        and lon == BASE * BASE
+        and NLON == 4 * lon
+        and m_dev % 128 == 0
+        and legendre.shape[2] == n_blk * 128
+        and cyc % n_blk == 0
+        and slots % 8 == 0
+    )
 
 
 def twiddle(first, count):
@@ -94,6 +576,13 @@
 
 def solution(mesh):
     placed = (P(None, "blk", "order"), P("blk", "order"), P(), P("blk", "order", None))
-    return jax.shard_map(
-        body, mesh=mesh, in_specs=placed, out_specs=P("blk", None, None, "order"), check_vma=False
-    )
+
+    def run(field, ocean_mask, plan, legendre):
+        chosen = fused_body if fits(mesh, field, legendre) else body
+        mapped = jax.shard_map(
+            chosen, mesh=mesh, in_specs=placed, out_specs=P("blk", None, None, "order"),
+            check_vma=False,
+        )
+        return mapped(field, ocean_mask, plan, legendre)
+
+    return run

time: 474 us -> 246 us (0.52); the launches traced: 464 us -> 246 us
  waiting for transfers between devices: 319 us -> 0 us
  Pallas kernels: 0 us -> 234 us
  matrix products: 57.3 us -> 0 us
  local copies, waits for them, and re-layouts: 32.3 us -> 8.59 us
  other arithmetic: 26 us -> 2.71 us
  starting transfers between devices: 15.5 us -> 0 us
  between operations: 14.1 us -> 0.03 us
    pallas_call x0 -> x1, Pallas kernels: none -> 234 us  [fused_body(): pl.pallas_call(functools.partial(fused_kernel, dims), out_shape=[jax.Shap...]
    ppermute x7 -> x0, waiting for transfers between devices: 207 us -> none  [the longest x4 157 us: pair_sum(): taken = lax.ppermute(given, 'blk', swap)]
    all_to_all x1 -> x0, waiting for transfers between devices: 71.3 us -> none  [pack_cycles(): lax.all_to_all(outgoing, 'blk', split_axis=1, concat_axis=1, tiled=True)]
    dot_general x12 -> x0, matrix products: 57.3 us -> none  [the longest x1 23.8 us: transform(): jnp.einsum('frn,ncm->frcm', values, table, precision=lax.Precision.HIGHEST)]
    reduce_scatter x1 -> x0, waiting for transfers between devices: 40.5 us -> none  [body(): lax.psum_scatter(terms, 'order', scatter_dimension=3, tiled=True)]
    mul x2 -> x1, other arithmetic: 19 us -> 0.01 us  [plan_maps(): jnp.arange(n_blk, dtype=jnp.int32)[:, None] * cap + rank]
    dynamic_slice x1 -> x0, local copies, waits for them, and re-layouts: 18.5 us -> none  [terms_for(): lax.dynamic_slice_in_dim(legendre, target * degree_dev, degree_dev, 2)]
    ppermute x7 -> x0, starting transfers between devices: 9.15 us -> none  [the longest x3 4.84 us: degree_sums(): lax.ppermute(pair_sum(step).astype(jnp.bfloat16), 'blk', shift)]
  transfers between devices with their start and end apart: 9 -> 0, of which waited for: 8 -> 0; matrix products, arithmetic and copies ran while one was open for 12% -> 0% of each run, Pallas kernels for 0% -> 0%
where the time goes in v1:
time: 246 us
  Pallas kernels  234 us (95%)
  local copies, waits for them, and re-layouts  8.59 us (3%)
  other arithmetic  2.71 us (1%)
    pallas_call x1, Pallas kernels, fused_body(): pl.pallas_call(functools.partial(fused_kernel, dims), out_shape=[jax.Shap...  234 us
    reshape x1, local copies, waits for them, and re-layouts, fused_body(): sums = sums.reshape(fields, 2, m_dev, l_dev)  7.19 us

profile of v1, /device:TPU:8, one launch (start us, length us, event | category | flops | bytes accessed | tf_op | source)
XLA Modules:
  0.0 245.6 jit_solution(11893592358638619448)
XLA Ops:
  0.0 0.7 fusion.4
  0.7 0.1 and.38
  0.8 0.7 broadcast_divide_fusion
  1.5 0.1 div.26
  1.6 0.3 convert_reduce_fusion
  1.9 0.1 broadcast_add_fusion
  2.0 0.1 add.52
  2.1 0.9 select_reduce_fusion
  3.0 0.6 broadcast_in_dim.16.recv_lanes
  3.6 0.6 broadcast_in_dim_tile.3.send_lanes
  4.1 234.3 %analysis.1 = (f32[8,4,256,128]{3,2,1,0:T(8,128)}, f32[16,64,1024]{2,1,0:T(8,128)}) custom-call(f32[16,64,1024]{2,1,0:T(8,128)} %field.1, s32[64,1024]{1,0:T(8,128)} %mask.1, bf16[48,256,1024]{2,1,0:T(8,128)(2,1)} %legendre.1, f32[4,4,32,256]{3,2,1,0:T(8,128)} %constant.42.clone.table, s32[1,128]{1,0:T(1,128)} %broadcast_in_dim_tile.3.send_lanes, ...), custom_call_target="tpu_custom_call" | custom-call | tf_op jit(solution)/shard_map/analysis/pallas_call | solution.py:457
  238.4 7.2 %copy.7 = f32[16,2,256,128]{2,1,0,3:T(2,128)} copy(f32[16,2,256,128]{3,2,1,0:T(8,128)} %bitcast.4) | data formatting | bytes 8388608 | tf_op jit(solution)/shard_map/reshape | solution.py:471
  (6 shorter events, 0.0 us)

commit v2 on v1

--- a/solution.py
+++ b/solution.py
@@ -34,37 +34,18 @@
     return stacked.transpose(2, 0, 1, 3).astype(np.float32)
 
 
-def plan_maps(plan, cycle_dev, slot_dev, orders_tile):
-    n_blk = lax.axis_size("blk")
-    own_index = lax.axis_index("blk")
-    cap = (cycle_dev + n_blk - 1) // n_blk
-    grid = plan.reshape(n_blk, cycle_dev)
-    owner = grid // slot_dev
-    positions = jnp.arange(cycle_dev, dtype=jnp.int32)
-    earlier = positions[None, :] < positions[:, None]
-    same_owner = owner[:, :, None] == owner[:, None, :]
-    rank = jnp.sum(same_owner & earlier[None], axis=2, dtype=jnp.int32)
-    send_pos = owner * cap + rank
-    local_pos = lax.dynamic_index_in_dim(send_pos, own_index, 0, keepdims=False)
-    source_pos = (jnp.arange(n_blk, dtype=jnp.int32)[:, None] * cap + rank).reshape(-1)
-    lanes = jnp.arange(slot_dev * orders_tile, dtype=jnp.int32) // orders_tile
-    wanted = own_index * slot_dev + lanes
-    hit = plan.reshape(-1)[:, None] == wanted[None, :]
-    received = jnp.sum(jnp.where(hit, source_pos[:, None], 0), axis=0, dtype=jnp.int32)
-    return jnp.tile(local_pos, CHUNK)[None, :], received[None, :]
-
-
 def fused_kernel(
     dims,
-    field, mask, legendre, table, send_lanes, recv_lanes,
+    field, mask, legendre, table, plan,
     out, far_field,
-    leg, spread, own_part, xs, xr, zr, wh, wl, near, far, mask_near, mask_far, parts,
+    leg, spread, own_part, far_part, xs, xr, zr, zbs, zbr, xbs, xbr, wh, wl, near, far, mask_near, mask_far, parts,
     y_own, y_send, y_recv, a_send, a_recv, pick, pack, stage, tabs,
     leg_sem, near_sem, far_sem, mask_sem, tab_sem, out_sem,
     pf_send, pf_recv, pm_send, pm_recv, ys_sem, yr_sem, as_sem, ar_sem,
-    xs_sem, xr_sem, zs_sem, zr_sem,
+    xs_sem, xr_sem, zs_sem, zr_sem, zbs_sem, zbr_sem, xbs_sem, xbr_sem,
 ):
-    n, groups, tile, m_dev, l_dev, cyc, lon, slot_dev, cap = dims
+    n, groups, x_groups, tile, m_dev, l_dev, cyc, lon, slot_dev, cap = dims
+    m_x = x_groups * tile
     rows = CHUNK * cyc
     n_blk = LINE * PAIR
     b = lax.axis_index("blk")
@@ -117,6 +98,11 @@
             field.at[fields], far_field.at[fields], pf_send.at[h], pf_recv.at[h], b, c_peer
         )
 
+    def push_first():
+        return remote(
+            field.at[pl.ds(0, CHUNK)], far.at[0], pf_send.at[0], pf_recv.at[0], b, c_peer
+        )
+
     tab_own = pltpu.make_async_copy(table.at[o], tabs.at[0], tab_sem.at[0])
     tab_other = pltpu.make_async_copy(table.at[y_peer], tabs.at[1], tab_sem.at[1])
     tab_own.start()
@@ -130,33 +116,51 @@
         pl.semaphore_signal(barrier, inc=1, device_id=((b + k) % n_blk, o), device_id_type=MESH)
     pl.semaphore_signal(barrier, inc=1, device_id=(b, y_peer), device_id_type=MESH)
     pl.semaphore_signal(barrier, inc=1, device_id=(b, c_peer), device_id_type=MESH)
+
+    def iota(shape, axis):
+        return lax.broadcasted_iota(jnp.int32, shape, axis)
+
+    wanted = (b * slot_dev + iota((1, slot_dev * tile), 1) // tile).astype(F32)
+    row_id, col_id = iota((cyc, cyc), 0), iota((cyc, cyc), 1)
+    send_at = jnp.zeros((1, cyc), F32)
+    source = jnp.zeros((cyc, slot_dev * tile), F32)
+    for block in range(n_blk):
+        across = plan[pl.ds(block, 1), :].astype(F32)
+        down = jnp.sum(jnp.where(row_id == col_id, across, 0.0), axis=1, keepdims=True)
+        owner_across = jnp.floor((across + 0.5) * (1.0 / slot_dev))
+        owner_down = jnp.floor((down + 0.5) * (1.0 / slot_dev))
+        same = owner_down == owner_across
+        rank_across = jnp.sum(
+            jnp.where(same & (row_id < col_id), 1.0, 0.0), axis=0, keepdims=True
+        )
+        rank_down = jnp.sum(
+            jnp.where(same & (col_id < row_id), 1.0, 0.0), axis=1, keepdims=True
+        )
+        here = jnp.where(b == block, 1.0, 0.0)
+        send_at += here * (owner_across * cap + rank_across)
+        source += jnp.where(down == wanted, block * cap + rank_down, 0.0)
+    source = jnp.sum(source, axis=0, keepdims=True)
+    per = CHUNK * cap
+    r = iota((rows, cyc), 0)
+    position = (r // per * cap + r % cap).astype(F32)
+    for f in range(CHUNK):
+        hit = (position == send_at) & (r % per // cap == f)
+        pack[:, pl.ds(f * cyc, cyc)] = jnp.where(hit, 1.0, 0.0).astype(BF16)
+    r = iota((rows, slot_dev * tile), 0)
+    position = (r // per * cap + r % cap).astype(F32)
+    for f in range(CHUNK):
+        hit = (position == source) & (r % per // cap == f)
+        pick[f] = jnp.where(hit, 1.0, 0.0).astype(BF16)
+
     pl.semaphore_wait(barrier, n_blk + 1)
 
     push_mask = remote(mask, mask_far, pm_send, pm_recv, b, c_peer)
     push_mask.start()
-
-    @pl.loop(0, n)
+    push_first().start()
+
+    @pl.loop(1, n)
     def _(h):
         push_field(h).start()
-
-    for half in (1, 0):
-        for j in range(LINE):
-            leg_copy(half, j).start()
-
-    def iota(shape, axis):
-        return lax.broadcasted_iota(jnp.int32, shape, axis)
-
-    r = iota((rows, rows), 0)
-    lane = iota((rows, rows), 1)
-    per = CHUNK * cap
-    position = r // per * cap + r % cap
-    hit = (position == send_lanes[...]) & (r % per // cap == lane // cyc)
-    pack[...] = jnp.where(hit, 1.0, 0.0).astype(BF16)
-    r = iota((rows, slot_dev * tile), 0)
-    position = r // per * cap + r % cap
-    for f in range(CHUNK):
-        hit = (position == recv_lanes[...]) & (r % per // cap == f)
-        pick[f] = jnp.where(hit, 1.0, 0.0).astype(BF16)
 
     tab_own.wait()
     tab_other.wait()
@@ -177,8 +181,6 @@
 
     mask_own.wait()
     push_mask.wait_recv()
-    push_field(0).wait_recv()
-    far_copy(0).start()
 
     def turn(index):
         quarter = (index * iota((1, m_dev), 1)) % 4
@@ -191,7 +193,17 @@
 
     def transform(h):
         near_copy(h).wait()
-        far_copy(h).wait()
+
+        @pl.when(h == 0)
+        def _():
+            push_first().wait_recv()
+            for half in (1, 0):
+                for j in range(LINE):
+                    leg_copy(half, j).start()
+
+        @pl.when(h > 0)
+        def _():
+            far_copy(h).wait()
 
         @pl.when(h + 1 < n)
         def _():
@@ -269,6 +281,59 @@
         table_part = leg[half, :, at, :].reshape(slot_dev * tile, LINE * l_dev)
         return at, jnp.dot(spread[g], table_part, preferred_element_type=F32)
 
+    def low_end_copy(h):
+        return remote(
+            zbs.at[h], zbr.at[h, pl.ds(0, LINE - 1)], zbs_sem.at[h, 0], zbr_sem.at[h, 0],
+            mate * PAIR + x, o,
+        )
+
+    def low_inner_copy(h, j):
+        to_z = (mate, far_end, far_inner)[j]
+        return remote(
+            zbs.at[h, j], zbr.at[h, (0, 1, 3)[j]], zbs_sem.at[h, j],
+            zbr_sem.at[h, (0, 1, 1)[j]], to_z * PAIR + x, o,
+        )
+
+    def low_x_copy(h):
+        return remote(xbs.at[h], xbr.at[h], xbs_sem.at[h], xbr_sem.at[h], x_peer, o)
+
+    def low_part(h, j, half):
+        if half == 0:
+            return own_part[h % 3, j, :, pl.ds(m_x, m_dev - m_x), :]
+        return far_part[h % 3, j]
+
+    def low_middle(h):
+        @pl.when(is_end == 0)
+        def _():
+            low_end_copy(h).wait_recv()
+            for j in (1, 2):
+                for half in range(2):
+                    value = low_part(h, j, half) + zbr[h, j - 1, half].astype(F32)
+                    zbs[h, j, half] = value.astype(BF16)
+                low_inner_copy(h, j).start()
+
+    def low_across(h):
+        def add(first, second):
+            for half in (1, 0):
+                value = low_part(h, LINE - 1, half)
+                value += zbr[h, first, half].astype(F32) + zbr[h, second, half].astype(F32)
+                if half == 0:
+                    own_part[h % 3, LINE - 1, :, pl.ds(m_x, m_dev - m_x), :] = value
+                else:
+                    xbs[h] = value.astype(BF16)
+            low_x_copy(h).start()
+
+        @pl.when(is_end == 1)
+        def _():
+            low_inner_copy(h, 0).wait_recv()
+            low_inner_copy(h, 1).wait_recv()
+            add(0, 1)
+
+        @pl.when(is_end == 0)
+        def _():
+            low_inner_copy(h, 2).wait_recv()
+            add(2, 3)
+
     def products(h):
         @pl.when(h == 0)
         def _():
@@ -280,7 +345,7 @@
             for j in range(LINE):
                 x_copy(h - 2, j).wait_send()
 
-        @pl.loop(0, groups)
+        @pl.loop(0, x_groups)
         def _(g):
             at, value = product(g, 1)
             for j in range(LINE):
@@ -295,7 +360,29 @@
             for j in range(LINE):
                 leg_copy(0, j).wait()
 
-        @pl.loop(0, groups)
+        @pl.loop(x_groups, groups)
+        def _(g):
+            low = pl.ds(pl.multiple_of((g - x_groups) * tile, tile), tile)
+            for half in range(2):
+                at, value = product(g, half)
+                for j in range(LINE):
+                    piece = value[:, j * l_dev : (j + 1) * l_dev].reshape(2 * CHUNK, tile, l_dev)
+                    if half == 0:
+                        own_part[h % 3, j, :, at, :] = piece
+                    else:
+                        far_part[h % 3, j, :, low, :] = piece
+                    if j < LINE - 1:
+                        zbs[h, j, half, :, low, :] = piece.astype(BF16)
+
+        @pl.when(is_end == 1)
+        def _():
+            low_end_copy(h).start()
+
+        @pl.when(is_end == 0)
+        def _():
+            low_inner_copy(h, 0).start()
+
+        @pl.loop(0, x_groups)
         def _(g):
             at, value = product(g, 0)
             for j in range(LINE):
@@ -314,12 +401,14 @@
     def inner_copy(h, j):
         return z_copy(h, j, (mate, far_end, far_inner)[j], (0, 1, 3)[j])
 
+    high = pl.ds(0, m_x)
+
     def first_sums(h):
         for j in range(LINE):
             x_copy(h, j).wait_recv()
-            value = own_part[h % 3, j] + xr[h % 5, j].astype(F32)
+            value = own_part[h % 3, j, :, high, :] + xr[h % 5, j].astype(F32)
             if j == LINE - 1:
-                own_part[h % 3, j] = value
+                own_part[h % 3, j, :, high, :] = value
                 continue
 
             @pl.when(is_end == 1)
@@ -331,17 +420,9 @@
             def _():
                 if j == 0:
                     xr[h % 5, j] = value.astype(BF16)
-                    inner_copy(h, j).start()
                 else:
-                    own_part[h % 3, j] = value
-
-    def second_sums(h):
-        @pl.when(is_end == 0)
-        def _():
-            for j in (1, 2):
-                end_copy(h, j - 1).wait_recv()
-                value = own_part[h % 3, j] + zr[h % 4, j - 1].astype(F32)
-                xr[h % 5, j] = value.astype(BF16)
+                    end_copy(h, j - 1).wait_recv()
+                    xr[h % 5, j] = (value + zr[h % 4, j - 1].astype(F32)).astype(BF16)
                 inner_copy(h, j).start()
 
     def out_copy(h):
@@ -352,22 +433,33 @@
         def _():
             out_copy(h - 2).wait()
 
+        def add(first, second):
+            value = own_part[h % 3, LINE - 1, :, high, :]
+            value += zr[h % 4, first].astype(F32) + zr[h % 4, second].astype(F32)
+            stage[h % 2, :, high, :] = value
+
         @pl.when(is_end == 1)
         def _():
             inner_copy(h, 0).wait_recv()
             inner_copy(h, 1).wait_recv()
-            stage[h % 2] = own_part[h % 3, 3] + zr[h % 4, 0].astype(F32) + zr[h % 4, 1].astype(F32)
-            for j in range(3):
+            add(0, 1)
+            for j in range(LINE - 1):
                 end_copy(h, j).wait_send()
+            low_end_copy(h).wait_send()
 
         @pl.when(is_end == 0)
         def _():
             end_copy(h, 2).wait_recv()
             inner_copy(h, 2).wait_recv()
-            stage[h % 2] = own_part[h % 3, 3] + zr[h % 4, 2].astype(F32) + zr[h % 4, 3].astype(F32)
-            for j in range(3):
+            add(2, 3)
+            for j in range(LINE - 1):
                 inner_copy(h, j).wait_send()
-
+                low_inner_copy(h, j).wait_send()
+
+        low_x_copy(h).wait_recv()
+        low = pl.ds(m_x, m_dev - m_x)
+        stage[h % 2, :, low, :] = own_part[h % 3, LINE - 1, :, low, :] + xbr[h].astype(F32)
+        low_x_copy(h).wait_send()
         out_copy(h).start()
 
     @pl.loop(0, n + 5)
@@ -378,18 +470,24 @@
                 step(t - delay)
 
         when(last_sums, 5)
+        when(low_across, 4)
         when(transform, 0)
         when(exchange, 1)
         when(spread_out, 2)
         when(products, 2)
-        when(second_sums, 4)
+        when(low_middle, 3)
         when(first_sums, 3)
 
     push_mask.wait_send()
+
+    push_first().wait_send()
+
+    @pl.loop(1, n)
+    def _(h):
+        push_field(h).wait_send()
 
     @pl.loop(0, n)
     def _(h):
-        push_field(h).wait_send()
         for k in range(1, n_blk):
             a_copy(h, k).wait_send()
 
@@ -411,9 +509,11 @@
     rows = CHUNK * cyc
     cap = (cyc + n_blk - 1) // n_blk
     per = CHUNK * cap
-    send_lanes, recv_lanes = plan_maps(plan, cyc, slot_dev, tile)
     table = jnp.asarray(table_of(lon, m_dev))
+    x_groups = groups - max(groups // 8, 1)
     piece = (2 * CHUNK, m_dev, l_dev)
+    high = (2 * CHUNK, x_groups * tile, l_dev)
+    low = (2 * CHUNK, m_dev - x_groups * tile, l_dev)
     dma = pltpu.SemaphoreType.DMA
     any_spec = pl.BlockSpec(memory_space=pl.ANY)
     vmem_spec = pl.BlockSpec(memory_space=pltpu.VMEM)
@@ -421,9 +521,14 @@
         pltpu.VMEM((2, slot_dev, m_dev, LINE * l_dev), BF16),
         pltpu.VMEM((groups, 2 * CHUNK * tile, slot_dev * tile), BF16),
         pltpu.VMEM((3, LINE) + piece, F32),
-        pltpu.VMEM((2, LINE) + piece, BF16),
-        pltpu.VMEM((5, LINE) + piece, BF16),
-        pltpu.VMEM((4, 4) + piece, BF16),
+        pltpu.VMEM((3, LINE) + low, F32),
+        pltpu.VMEM((2, LINE) + high, BF16),
+        pltpu.VMEM((5, LINE) + high, BF16),
+        pltpu.VMEM((4, 4) + high, BF16),
+        pltpu.VMEM((n, LINE - 1, 2) + low, BF16),
+        pltpu.VMEM((n, 4, 2) + low, BF16),
+        pltpu.VMEM((n,) + low, BF16),
+        pltpu.VMEM((n,) + low, BF16),
         pltpu.VMEM((2, lon, 2 * m_dev), BF16),
         pltpu.VMEM((2, lon, 2 * m_dev), BF16),
         pltpu.VMEM((2, CHUNK, cyc, lon), F32),
@@ -452,22 +557,24 @@
         dma((n, n_blk - 1)), dma((n, n_blk - 1)),
         dma((2, LINE)), dma((n, LINE)),
         dma((n, 3)), dma((n, 4)),
+        dma((n, 3)), dma((n, 2)),
+        dma((n,)), dma((n,)),
     ]
-    dims = (n, groups, tile, m_dev, l_dev, cyc, lon, slot_dev, cap)
+    dims = (n, groups, x_groups, tile, m_dev, l_dev, cyc, lon, slot_dev, cap)
     sums, _ = pl.pallas_call(
         functools.partial(fused_kernel, dims),
         out_shape=[
             jax.ShapeDtypeStruct((n,) + piece, F32),
             jax.ShapeDtypeStruct(field.shape, F32),
         ],
-        in_specs=[any_spec] * 4 + [vmem_spec] * 2,
+        in_specs=[any_spec] * 4 + [vmem_spec],
         out_specs=[any_spec] * 2,
         scratch_shapes=scratch,
         compiler_params=pltpu.CompilerParams(
             collective_id=0, has_side_effects=True, vmem_limit_bytes=66 * 1000 * 1000
         ),
         name="analysis",
-    )(field, ocean_mask, legendre, table, send_lanes, recv_lanes)
+    )(field, ocean_mask, legendre, table, plan.reshape(n_blk, cyc))
     sums = sums.reshape(fields, 2, m_dev, l_dev)
     return jnp.transpose(sums, (3, 0, 1, 2))
 

time: 246 us -> 219 us (0.89)
  Pallas kernels: 234 us -> 208 us
  other arithmetic: 2.71 us -> 0 us
    pallas_call x1, Pallas kernels: 234 us -> 208 us  [fused_body(): pl.pallas_call(functools.partial(fused_kernel, dims), out_shape=[jax.Shap...]
where the time goes in v2:
time: 219 us; the launch traced here: 217 us
  Pallas kernels  208 us (95%)
  local copies, waits for them, and re-layouts  8.54 us (4%)
    pallas_call x1, Pallas kernels, fused_body(): pl.pallas_call(functools.partial(fused_kernel, dims), out_shape=[jax.Shap...  208 us
    reshape x1, local copies, waits for them, and re-layouts, fused_body(): sums = sums.reshape(fields, 2, m_dev, l_dev)  7.19 us

profile of v2, /device:TPU:8, one launch (start us, length us, event | category | flops | bytes accessed | tf_op | source)
XLA Modules:
  0.0 216.6 jit_solution(1736045142844957745)
XLA Ops:
  0.0 1.3 reshape.6.plan
  1.3 208.1 %analysis.1 = (f32[8,4,256,128]{3,2,1,0:T(8,128)}, f32[16,64,1024]{2,1,0:T(8,128)}) custom-call(f32[16,64,1024]{2,1,0:T(8,128)} %field.1, s32[64,1024]{1,0:T(8,128)} %mask.1, bf16[48,256,1024]{2,1,0:T(8,128)(2,1)} %legendre.1, f32[4,4,32,256]{3,2,1,0:T(8,128)} %constant.2.clone.table, s32[8,64]{1,0:T(8,128)} %reshape.6.plan), custom_call_target="tpu_custom_call" | custom-call | tf_op jit(solution)/shard_map/analysis/pallas_call | solution.py:564
  209.4 7.2 %copy.6 = f32[16,2,256,128]{2,1,0,3:T(2,128)} copy(f32[16,2,256,128]{3,2,1,0:T(8,128)} %bitcast.2) | data formatting | bytes 8388608 | tf_op jit(solution)/shard_map/reshape | solution.py:578

commit v3 on v2

--- a/solution.py
+++ b/solution.py
@@ -98,9 +98,9 @@
             field.at[fields], far_field.at[fields], pf_send.at[h], pf_recv.at[h], b, c_peer
         )
 
-    def push_first():
+    def push_first(h):
         return remote(
-            field.at[pl.ds(0, CHUNK)], far.at[0], pf_send.at[0], pf_recv.at[0], b, c_peer
+            field.at[pl.ds(h * CHUNK, CHUNK)], far.at[h], pf_send.at[h], pf_recv.at[h], b, c_peer
         )
 
     tab_own = pltpu.make_async_copy(table.at[o], tabs.at[0], tab_sem.at[0])
@@ -110,6 +110,7 @@
     mask_own = pltpu.make_async_copy(mask, mask_near, mask_sem)
     mask_own.start()
     near_copy(0).start()
+    near_copy(1).start()
 
     barrier = pltpu.get_barrier_semaphore()
     for k in range(1, n_blk):
@@ -156,9 +157,10 @@
 
     push_mask = remote(mask, mask_far, pm_send, pm_recv, b, c_peer)
     push_mask.start()
-    push_first().start()
-
-    @pl.loop(1, n)
+    push_first(0).start()
+    push_first(1).start()
+
+    @pl.loop(2, n)
     def _(h):
         push_field(h).start()
 
@@ -180,7 +182,7 @@
                 wl[side_of, at, pl.ds(c * m_dev, m_dev)] = rest.astype(BF16)
 
     mask_own.wait()
-    push_mask.wait_recv()
+    push_mask.wait()
 
     def turn(index):
         quarter = (index * iota((1, m_dev), 1)) % 4
@@ -194,21 +196,24 @@
     def transform(h):
         near_copy(h).wait()
 
+        @pl.when(h < 2)
+        def _():
+            push_first(h).wait()
+
         @pl.when(h == 0)
         def _():
-            push_first().wait_recv()
             for half in (1, 0):
                 for j in range(LINE):
                     leg_copy(half, j).start()
 
-        @pl.when(h > 0)
+        @pl.when(h >= 2)
         def _():
             far_copy(h).wait()
 
-        @pl.when(h + 1 < n)
+        @pl.when((h >= 1) & (h + 1 < n))
         def _():
             near_copy(h + 1).start()
-            push_field(h + 1).wait_recv()
+            push_field(h + 1).wait()
             far_copy(h + 1).start()
 
         @pl.when(h >= 2)
@@ -258,7 +263,7 @@
 
     def spread_out(h):
         for k in range(1, n_blk):
-            a_copy(h, k).wait_recv()
+            a_copy(h, k).wait()
         got = a_recv[h].reshape(rows, 2 * m_dev)
         for c in range(2):
             for f in range(CHUNK):
@@ -276,9 +281,10 @@
             xs.at[h % 2, j], xr.at[h % 5, j], xs_sem.at[h % 2, j], xr_sem.at[h, j], x_peer, o
         )
 
-    def product(g, half):
+    def product(g, half, first=0, count=LINE):
         at = pl.ds(pl.multiple_of(g * tile, tile), tile)
-        table_part = leg[half, :, at, :].reshape(slot_dev * tile, LINE * l_dev)
+        lanes = pl.ds(first * l_dev, count * l_dev)
+        table_part = leg[half, :, at, lanes].reshape(slot_dev * tile, count * l_dev)
         return at, jnp.dot(spread[g], table_part, preferred_element_type=F32)
 
     def low_end_copy(h):
@@ -345,15 +351,25 @@
             for j in range(LINE):
                 x_copy(h - 2, j).wait_send()
 
-        @pl.loop(0, x_groups)
-        def _(g):
-            at, value = product(g, 1)
-            for j in range(LINE):
-                piece = value[:, j * l_dev : (j + 1) * l_dev].reshape(2 * CHUNK, tile, l_dev)
-                xs[h % 2, j, :, at, :] = piece.astype(BF16)
-
-        for j in range(LINE):
-            x_copy(h, j).start()
+        def x_products(first, count):
+            @pl.loop(0, x_groups)
+            def _(g):
+                at, value = product(g, 1, first, count)
+                for j in range(count):
+                    piece = value[:, j * l_dev : (j + 1) * l_dev].reshape(2 * CHUNK, tile, l_dev)
+                    xs[h % 2, first + j, :, at, :] = piece.astype(BF16)
+
+            for j in range(count):
+                x_copy(h, first + j).start()
+
+        @pl.when(h == 0)
+        def _():
+            x_products(0, 2)
+            x_products(2, 2)
+
+        @pl.when(h > 0)
+        def _():
+            x_products(0, LINE)
 
         @pl.when(h == 0)
         def _():
@@ -405,6 +421,12 @@
 
     def first_sums(h):
         for j in range(LINE):
+            if j == LINE - 1:
+
+                @pl.when(h == n - 1)
+                def _():
+                    low_across(h)
+
             x_copy(h, j).wait_recv()
             value = own_part[h % 3, j, :, high, :] + xr[h % 5, j].astype(F32)
             if j == LINE - 1:
@@ -470,26 +492,17 @@
                 step(t - delay)
 
         when(last_sums, 5)
-        when(low_across, 4)
+
+        @pl.when((t >= 4) & (t < n + 3))
+        def _():
+            low_across(t - 4)
+
         when(transform, 0)
         when(exchange, 1)
         when(spread_out, 2)
         when(products, 2)
         when(low_middle, 3)
         when(first_sums, 3)
-
-    push_mask.wait_send()
-
-    push_first().wait_send()
-
-    @pl.loop(1, n)
-    def _(h):
-        push_field(h).wait_send()
-
-    @pl.loop(0, n)
-    def _(h):
-        for k in range(1, n_blk):
-            a_copy(h, k).wait_send()
 
     for h in (n - 2, n - 1):
         y_copy(h).wait_send()

time: 219 us -> 213 us (0.973)
  Pallas kernels: 208 us -> 204 us
    pallas_call x1, Pallas kernels: 208 us -> 204 us  [fused_body(): pl.pallas_call(functools.partial(fused_kernel, dims), out_shape=[jax.Shap...]
where the time goes in v3:
time: 213 us
  Pallas kernels  204 us (96%)
  local copies, waits for them, and re-layouts  8.54 us (4%)
    pallas_call x1, Pallas kernels, fused_body(): pl.pallas_call(functools.partial(fused_kernel, dims), out_shape=[jax.Shap...  204 us
    reshape x1, local copies, waits for them, and re-layouts, fused_body(): sums = sums.reshape(fields, 2, m_dev, l_dev)  7.19 us

profile of v3, /device:TPU:8, one launch (start us, length us, event | category | flops | bytes accessed | tf_op | source)
XLA Modules:
  0.0 212.6 jit_solution(1057797714041106802)
XLA Ops:
  0.0 1.3 reshape.6.plan
  1.3 204.1 %analysis.1 = (f32[8,4,256,128]{3,2,1,0:T(8,128)}, f32[16,64,1024]{2,1,0:T(8,128)}) custom-call(f32[16,64,1024]{2,1,0:T(8,128)} %field.1, s32[64,1024]{1,0:T(8,128)} %mask.1, bf16[48,256,1024]{2,1,0:T(8,128)(2,1)} %legendre.1, f32[4,4,32,256]{3,2,1,0:T(8,128)} %constant.2.clone.table, s32[8,64]{1,0:T(8,128)} %reshape.6.plan), custom_call_target="tpu_custom_call" | custom-call | tf_op jit(solution)/shard_map/analysis/pallas_call | solution.py:577
  205.4 7.2 %copy.6 = f32[16,2,256,128]{2,1,0,3:T(2,128)} copy(f32[16,2,256,128]{3,2,1,0:T(8,128)} %bitcast.2) | data formatting | bytes 8388608 | tf_op jit(solution)/shard_map/reshape | solution.py:591

commit v4 on v3

--- a/solution.py
+++ b/solution.py
@@ -126,7 +126,7 @@
     send_at = jnp.zeros((1, cyc), F32)
     source = jnp.zeros((cyc, slot_dev * tile), F32)
     for block in range(n_blk):
-        across = plan[pl.ds(block, 1), :].astype(F32)
+        across = plan[:, pl.ds(block * cyc, cyc)].astype(F32)
         down = jnp.sum(jnp.where(row_id == col_id, across, 0.0), axis=1, keepdims=True)
         owner_across = jnp.floor((across + 0.5) * (1.0 / slot_dev))
         owner_down = jnp.floor((down + 0.5) * (1.0 / slot_dev))
@@ -191,7 +191,7 @@
         return real, imag
 
     def y_copy(h):
-        return remote(y_send.at[h % 2], y_recv.at[h], ys_sem.at[h % 2], yr_sem.at[h], b, y_peer)
+        return remote(y_send.at[h % 2], y_recv.at[h], ys_sem.at[h % 2], yr_sem.at[h % 4], b, y_peer)
 
     def transform(h):
         near_copy(h).wait()
@@ -247,7 +247,7 @@
     def a_copy(h, k):
         to = (b + k) % n_blk
         return remote(
-            a_send.at[h, to], a_recv.at[h, b], as_sem.at[h, k - 1], ar_sem.at[h, k - 1], to, o
+            a_send.at[h, to], a_recv.at[h, b], as_sem.at[h % 4, k - 1], ar_sem.at[h % 4, k - 1], to, o
         )
 
     def exchange(h):
@@ -278,7 +278,7 @@
 
     def x_copy(h, j):
         return remote(
-            xs.at[h % 2, j], xr.at[h % 5, j], xs_sem.at[h % 2, j], xr_sem.at[h, j], x_peer, o
+            xs.at[h % 2, j], xr.at[h % 5, j], xs_sem.at[h % 2, j], xr_sem.at[h % 5, j], x_peer, o
         )
 
     def product(g, half, first=0, count=LINE):
@@ -289,19 +289,19 @@
 
     def low_end_copy(h):
         return remote(
-            zbs.at[h], zbr.at[h, pl.ds(0, LINE - 1)], zbs_sem.at[h, 0], zbr_sem.at[h, 0],
+            zbs.at[h], zbr.at[h, pl.ds(0, LINE - 1)], zbs_sem.at[h % 4, 0], zbr_sem.at[h % 4, 0],
             mate * PAIR + x, o,
         )
 
     def low_inner_copy(h, j):
         to_z = (mate, far_end, far_inner)[j]
         return remote(
-            zbs.at[h, j], zbr.at[h, (0, 1, 3)[j]], zbs_sem.at[h, j],
-            zbr_sem.at[h, (0, 1, 1)[j]], to_z * PAIR + x, o,
+            zbs.at[h, j], zbr.at[h, (0, 1, 3)[j]], zbs_sem.at[h % 4, j],
+            zbr_sem.at[h % 4, (0, 1, 1)[j]], to_z * PAIR + x, o,
         )
 
     def low_x_copy(h):
-        return remote(xbs.at[h], xbr.at[h], xbs_sem.at[h], xbr_sem.at[h], x_peer, o)
+        return remote(xbs.at[h], xbr.at[h], xbs_sem.at[h % 4], xbr_sem.at[h % 4], x_peer, o)
 
     def low_part(h, j, half):
         if half == 0:
@@ -359,17 +359,22 @@
                     piece = value[:, j * l_dev : (j + 1) * l_dev].reshape(2 * CHUNK, tile, l_dev)
                     xs[h % 2, first + j, :, at, :] = piece.astype(BF16)
 
+        def x_start(first, count):
             for j in range(count):
                 x_copy(h, first + j).start()
 
         @pl.when(h == 0)
         def _():
             x_products(0, 2)
+            exchange(1)
+            x_start(0, 2)
             x_products(2, 2)
+            x_start(2, 2)
 
         @pl.when(h > 0)
         def _():
             x_products(0, LINE)
+            x_start(0, LINE)
 
         @pl.when(h == 0)
         def _():
@@ -407,7 +412,7 @@
 
     def z_copy(h, j, to_z, slot):
         return remote(
-            xr.at[h % 5, j], zr.at[h % 4, slot], zs_sem.at[h, j], zr_sem.at[h, slot],
+            xr.at[h % 5, j], zr.at[h % 4, slot], zs_sem.at[h % 4, j], zr_sem.at[h % 4, slot],
             to_z * PAIR + x, o,
         )
 
@@ -448,7 +453,9 @@
                 inner_copy(h, j).start()
 
     def out_copy(h):
-        return pltpu.make_async_copy(stage.at[h % 2], out.at[h], out_sem.at[h % 2])
+        return pltpu.make_async_copy(
+            stage.at[h % 2], out.at[:, pl.ds(h * CHUNK, CHUNK)], out_sem.at[h % 2]
+        )
 
     def last_sums(h):
         @pl.when(h >= 2)
@@ -458,7 +465,7 @@
         def add(first, second):
             value = own_part[h % 3, LINE - 1, :, high, :]
             value += zr[h % 4, first].astype(F32) + zr[h % 4, second].astype(F32)
-            stage[h % 2, :, high, :] = value
+            own_part[h % 3, LINE - 1, :, high, :] = value
 
         @pl.when(is_end == 1)
         def _():
@@ -480,7 +487,10 @@
 
         low_x_copy(h).wait_recv()
         low = pl.ds(m_x, m_dev - m_x)
-        stage[h % 2, :, low, :] = own_part[h % 3, LINE - 1, :, low, :] + xbr[h].astype(F32)
+        own_part[h % 3, LINE - 1, :, low, :] += xbr[h].astype(F32)
+        for f in range(CHUNK):
+            for c in range(2):
+                stage[h % 2, :, f, c, :] = own_part[h % 3, LINE - 1, 2 * f + c].T
         low_x_copy(h).wait_send()
         out_copy(h).start()
 
@@ -498,7 +508,11 @@
             low_across(t - 4)
 
         when(transform, 0)
-        when(exchange, 1)
+
+        @pl.when((t >= 1) & (t != 2) & (t < n + 1))
+        def _():
+            exchange(t - 1)
+
         when(spread_out, 2)
         when(products, 2)
         when(low_middle, 3)
@@ -556,7 +570,7 @@
         pltpu.VMEM((n, n_blk, per, 2 * m_dev), BF16),
         pltpu.VMEM((CHUNK, rows, slot_dev * tile), BF16),
         pltpu.VMEM((rows, rows), BF16),
-        pltpu.VMEM((2,) + piece, F32),
+        pltpu.VMEM((2, l_dev, CHUNK, 2, m_dev), F32),
         pltpu.VMEM((2, 4, BASE, m_dev), F32),
         dma((2, LINE)),
         dma((2,)),
@@ -566,18 +580,18 @@
         dma((2,)),
         dma((n,)), dma((n,)),
         dma, dma,
-        dma((2,)), dma((n,)),
-        dma((n, n_blk - 1)), dma((n, n_blk - 1)),
-        dma((2, LINE)), dma((n, LINE)),
-        dma((n, 3)), dma((n, 4)),
-        dma((n, 3)), dma((n, 2)),
-        dma((n,)), dma((n,)),
+        dma((2,)), dma((4,)),
+        dma((4, n_blk - 1)), dma((4, n_blk - 1)),
+        dma((2, LINE)), dma((5, LINE)),
+        dma((4, 3)), dma((4, 4)),
+        dma((4, 3)), dma((4, 2)),
+        dma((4,)), dma((4,)),
     ]
     dims = (n, groups, x_groups, tile, m_dev, l_dev, cyc, lon, slot_dev, cap)
     sums, _ = pl.pallas_call(
         functools.partial(fused_kernel, dims),
         out_shape=[
-            jax.ShapeDtypeStruct((n,) + piece, F32),
+            jax.ShapeDtypeStruct((l_dev, fields, 2, m_dev), F32),
             jax.ShapeDtypeStruct(field.shape, F32),
         ],
         in_specs=[any_spec] * 4 + [vmem_spec],
@@ -587,9 +601,37 @@
             collective_id=0, has_side_effects=True, vmem_limit_bytes=66 * 1000 * 1000
         ),
         name="analysis",
-    )(field, ocean_mask, legendre, table, plan.reshape(n_blk, cyc))
-    sums = sums.reshape(fields, 2, m_dev, l_dev)
-    return jnp.transpose(sums, (3, 0, 1, 2))
+    )(field, ocean_mask, legendre, table, plan.reshape(1, -1))
+    parts = 8
+    return pl.pallas_call(
+        hand_on_kernel,
+        out_shape=jax.ShapeDtypeStruct(sums.shape, F32),
+        in_specs=[any_spec],
+        out_specs=any_spec,
+        scratch_shapes=[
+            pltpu.VMEM((parts, l_dev // parts) + sums.shape[1:], F32),
+            dma((parts,)), dma((parts,)),
+        ],
+        name="hand_on",
+    )(sums)
+
+
+def hand_on_kernel(source, target, held, in_sem, out_sem):
+    parts, depth = held.shape[:2]
+
+    def into(k):
+        return pltpu.make_async_copy(source.at[pl.ds(k * depth, depth)], held.at[k], in_sem.at[k])
+
+    def away(k):
+        return pltpu.make_async_copy(held.at[k], target.at[pl.ds(k * depth, depth)], out_sem.at[k])
+
+    for k in range(parts):
+        into(k).start()
+    for k in range(parts):
+        into(k).wait()
+        away(k).start()
+    for k in range(parts):
+        away(k).wait()
 
 
 def fits(mesh, field, legendre):

time: 213 us -> 207 us (0.972)
  local copies, waits for them, and re-layouts: 8.54 us -> 0 us
  Pallas kernels: 204 us -> 207 us
    reshape x2 -> x0, local copies, waits for them, and re-layouts: 8.54 us -> none  [the longest x1 7.19 us: fused_body(): sums = sums.reshape(fields, 2, m_dev, l_dev)]
    pallas_call x0 -> x1, Pallas kernels: none -> 3.58 us  [fused_body(): pl.pallas_call(hand_on_kernel, out_shape=jax.ShapeDtypeStruct(sums.shape,...]
where the time goes in v4:
time: 207 us
  Pallas kernels  207 us (100%)
    pallas_call x1, Pallas kernels, fused_body(): pl.pallas_call(functools.partial(fused_kernel, dims), out_shape=[jax.Shap...  203 us

profile of v4, /device:TPU:8, one launch (start us, length us, event | category | flops | bytes accessed | tf_op | source)
XLA Modules:
  0.0 206.5 jit_solution(3163788874750164640)
XLA Ops:
  0.0 202.9 %analysis.1 = (f32[128,16,2,256]{3,2,1,0:T(2,128)}, f32[16,64,1024]{2,1,0:T(8,128)}) custom-call(f32[16,64,1024]{2,1,0:T(8,128)} %field.1, s32[64,1024]{1,0:T(8,128)} %mask.1, bf16[48,256,1024]{2,1,0:T(8,128)(2,1)} %legendre.1, f32[4,4,32,256]{3,2,1,0:T(8,128)} %constant.2.clone.table, s32[1,512]{1,0:T(1,128)} %bitcast.1), custom_call_target="tpu_custom_call" | custom-call | tf_op jit(solution)/shard_map/analysis/pallas_call | solution.py:591
  203.0 3.6 %hand_on.1 = f32[128,16,2,256]{3,2,1,0:T(2,128)} custom-call(f32[128,16,2,256]{3,2,1,0:T(2,128)} %get-tuple-element.6.source), custom_call_target="tpu_custom_call" | custom-call | tf_op jit(solution)/shard_map/hand_on/pallas_call | solution.py:606

commit v5 on v4

--- a/solution.py
+++ b/solution.py
@@ -39,10 +39,10 @@
     field, mask, legendre, table, plan,
     out, far_field,
     leg, spread, own_part, far_part, xs, xr, zr, zbs, zbr, xbs, xbr, wh, wl, near, far, mask_near, mask_far, parts,
-    y_own, y_send, y_recv, a_send, a_recv, pick, pack, stage, tabs,
+    y_own, y_send, y_recv, y_first, y_begun, a_send, a_recv, pick, pack, stage, tabs,
     leg_sem, near_sem, far_sem, mask_sem, tab_sem, out_sem,
     pf_send, pf_recv, pm_send, pm_recv, ys_sem, yr_sem, as_sem, ar_sem,
-    xs_sem, xr_sem, zs_sem, zr_sem, zbs_sem, zbr_sem, xbs_sem, xbr_sem,
+    xs_sem, xr_sem, zs_sem, zr_sem, zbs_sem, zbr_sem, xbs_sem, xbr_sem, yf_sem, yb_sem,
 ):
     n, groups, x_groups, tile, m_dev, l_dev, cyc, lon, slot_dev, cap = dims
     m_x = x_groups * tile
@@ -193,6 +193,8 @@
     def y_copy(h):
         return remote(y_send.at[h % 2], y_recv.at[h], ys_sem.at[h % 2], yr_sem.at[h % 4], b, y_peer)
 
+    first_y = remote(y_first, y_begun, yf_sem, yb_sem, b, y_peer)
+
     def transform(h):
         near_copy(h).wait()
 
@@ -202,9 +204,8 @@
 
         @pl.when(h == 0)
         def _():
-            for half in (1, 0):
-                for j in range(LINE):
-                    leg_copy(half, j).start()
+            for j in range(LINE):
+                leg_copy(1, j).start()
 
         @pl.when(h >= 2)
         def _():
@@ -216,7 +217,12 @@
             push_field(h + 1).wait()
             far_copy(h + 1).start()
 
-        @pl.when(h >= 2)
+        @pl.when(h == 1)
+        def _():
+            for j in range(LINE):
+                leg_copy(0, j).start()
+
+        @pl.when(h >= 3)
         def _():
             y_copy(h - 2).wait_send()
 
@@ -238,11 +244,23 @@
             fr, fi = total[rows:, :m_dev], total[rows:, m_dev:]
             real = near_r * nr - near_i * ni + far_r * fr - far_i * fi
             imag = near_r * ni + near_i * nr + far_r * fi + far_i * fr
-            target = y_send if side_of else y_own
-            target[h % 2, :, pl.ds(0, m_dev)] = real
-            target[h % 2, :, pl.ds(m_dev, m_dev)] = imag
             if side_of:
-                y_copy(h).start()
+
+                @pl.when(h == 0)
+                def _():
+                    y_first[:, pl.ds(0, m_dev)] = real.astype(BF16)
+                    y_first[:, pl.ds(m_dev, m_dev)] = imag.astype(BF16)
+                    first_y.start()
+
+                @pl.when(h > 0)
+                def _():
+                    y_send[h % 2, :, pl.ds(0, m_dev)] = real
+                    y_send[h % 2, :, pl.ds(m_dev, m_dev)] = imag
+                    y_copy(h).start()
+
+            else:
+                y_own[h % 2, :, pl.ds(0, m_dev)] = real
+                y_own[h % 2, :, pl.ds(m_dev, m_dev)] = imag
 
     def a_copy(h, k):
         to = (b + k) % n_blk
@@ -251,7 +269,15 @@
         )
 
     def exchange(h):
-        y_copy(h).wait_recv()
+        @pl.when(h == 0)
+        def _():
+            first_y.wait()
+            y_recv[h] = y_begun[...].astype(F32)
+
+        @pl.when(h > 0)
+        def _():
+            y_copy(h).wait_recv()
+
         spectrum = (y_own[h % 2] + y_recv[h]).astype(BF16)
         packed = jnp.dot(pack[...], spectrum, preferred_element_type=F32).astype(BF16)
         a_send[h] = packed.reshape(n_blk, per, 2 * m_dev)
@@ -566,6 +592,8 @@
         pltpu.VMEM((2, rows, 2 * m_dev), F32),
         pltpu.VMEM((2, rows, 2 * m_dev), F32),
         pltpu.VMEM((n, rows, 2 * m_dev), F32),
+        pltpu.VMEM((rows, 2 * m_dev), BF16),
+        pltpu.VMEM((rows, 2 * m_dev), BF16),
         pltpu.VMEM((n, n_blk, per, 2 * m_dev), BF16),
         pltpu.VMEM((n, n_blk, per, 2 * m_dev), BF16),
         pltpu.VMEM((CHUNK, rows, slot_dev * tile), BF16),
@@ -586,6 +614,7 @@
         dma((4, 3)), dma((4, 4)),
         dma((4, 3)), dma((4, 2)),
         dma((4,)), dma((4,)),
+        dma, dma,
     ]
     dims = (n, groups, x_groups, tile, m_dev, l_dev, cyc, lon, slot_dev, cap)
     sums, _ = pl.pallas_call(

time: 207 us -> 204 us (0.986)
  Pallas kernels: 207 us -> 204 us
    pallas_call x1, Pallas kernels: 203 us -> 200 us  [fused_body(): pl.pallas_call(functools.partial(fused_kernel, dims), out_shape=[jax.Shap...]
where the time goes in v5:
time: 204 us
  Pallas kernels  204 us (100%)
    pallas_call x1, Pallas kernels, fused_body(): pl.pallas_call(functools.partial(fused_kernel, dims), out_shape=[jax.Shap...  200 us

profile of v5, /device:TPU:8, one launch (start us, length us, event | category | flops | bytes accessed | tf_op | source)
XLA Modules:
  0.0 203.8 jit_solution(476627536366376403)
XLA Ops:
  0.0 200.2 %analysis.1 = (f32[128,16,2,256]{3,2,1,0:T(2,128)}, f32[16,64,1024]{2,1,0:T(8,128)}) custom-call(f32[16,64,1024]{2,1,0:T(8,128)} %field.1, s32[64,1024]{1,0:T(8,128)} %mask.1, bf16[48,256,1024]{2,1,0:T(8,128)(2,1)} %legendre.1, f32[4,4,32,256]{3,2,1,0:T(8,128)} %constant.2.clone.table, s32[1,512]{1,0:T(1,128)} %bitcast.1), custom_call_target="tpu_custom_call" | custom-call | tf_op jit(solution)/shard_map/analysis/pallas_call | solution.py:620
  200.2 3.6 %hand_on.1 = f32[128,16,2,256]{3,2,1,0:T(2,128)} custom-call(f32[128,16,2,256]{3,2,1,0:T(2,128)} %get-tuple-element.6.source), custom_call_target="tpu_custom_call" | custom-call | tf_op jit(solution)/shard_map/hand_on/pallas_call | solution.py:635

commit v6 on v5

--- a/solution.py
+++ b/solution.py
@@ -100,7 +100,7 @@
 
     def push_first(h):
         return remote(
-            field.at[pl.ds(h * CHUNK, CHUNK)], far.at[h], pf_send.at[h], pf_recv.at[h], b, c_peer
+            near.at[h], far.at[h], pf_send.at[h], pf_recv.at[h], b, c_peer
         )
 
     tab_own = pltpu.make_async_copy(table.at[o], tabs.at[0], tab_sem.at[0])
@@ -155,10 +155,12 @@
 
     pl.semaphore_wait(barrier, n_blk + 1)
 
-    push_mask = remote(mask, mask_far, pm_send, pm_recv, b, c_peer)
+    push_mask = remote(mask_near, mask_far, pm_send, pm_recv, b, c_peer)
+    mask_own.wait()
     push_mask.start()
-    push_first(0).start()
-    push_first(1).start()
+    for h in range(2):
+        near_copy(h).wait()
+        push_first(h).start()
 
     @pl.loop(2, n)
     def _(h):
@@ -181,7 +183,6 @@
                 rest = value - high.astype(F32)
                 wl[side_of, at, pl.ds(c * m_dev, m_dev)] = rest.astype(BF16)
 
-    mask_own.wait()
     push_mask.wait()
 
     def turn(index):
@@ -196,8 +197,6 @@
     first_y = remote(y_first, y_begun, yf_sem, yb_sem, b, y_peer)
 
     def transform(h):
-        near_copy(h).wait()
-
         @pl.when(h < 2)
         def _():
             push_first(h).wait()
@@ -209,6 +208,7 @@
 
         @pl.when(h >= 2)
         def _():
+            near_copy(h).wait()
             far_copy(h).wait()
 
         @pl.when((h >= 1) & (h + 1 < n))
@@ -400,7 +400,11 @@
         @pl.when(h > 0)
         def _():
             x_products(0, LINE)
-            x_start(0, LINE)
+            x_start(0, LINE - 1)
+
+            @pl.when(h < n - 1)
+            def _():
+                x_start(LINE - 1, 1)
 
         @pl.when(h == 0)
         def _():
@@ -457,6 +461,7 @@
                 @pl.when(h == n - 1)
                 def _():
                     low_across(h)
+                    last_sums(h - 1)
 
             x_copy(h, j).wait_recv()
             value = own_part[h % 3, j, :, high, :] + xr[h % 5, j].astype(F32)
@@ -527,11 +532,18 @@
             def _():
                 step(t - delay)
 
-        when(last_sums, 5)
+        @pl.when((t >= 5) & (t != n + 3) & (t < n + 5))
+        def _():
+            last_sums(t - 5)
+
 
         @pl.when((t >= 4) & (t < n + 3))
         def _():
             low_across(t - 4)
+
+        @pl.when(t == n + 2)
+        def _():
+            x_copy(n - 1, LINE - 1).start()
 
         when(transform, 0)
 

time: 204 us -> 204 us (level)
  no operation moved by 1% of the time
where the time goes in v6:
time: 204 us
  Pallas kernels  204 us (100%)
    pallas_call x1, Pallas kernels, fused_body(): pl.pallas_call(functools.partial(fused_kernel, dims), out_shape=[jax.Shap...  200 us

profile of v6, /device:TPU:8, one launch (start us, length us, event | category | flops | bytes accessed | tf_op | source)
XLA Modules:
  0.0 203.6 jit_solution(14590828741031094763)
XLA Ops:
  0.0 200.0 %analysis.1 = (f32[128,16,2,256]{3,2,1,0:T(2,128)}, f32[16,64,1024]{2,1,0:T(8,128)}) custom-call(f32[16,64,1024]{2,1,0:T(8,128)} %field.1, s32[64,1024]{1,0:T(8,128)} %mask.1, bf16[48,256,1024]{2,1,0:T(8,128)(2,1)} %legendre.1, f32[4,4,32,256]{3,2,1,0:T(8,128)} %constant.2.clone.table, s32[1,512]{1,0:T(1,128)} %bitcast.1), custom_call_target="tpu_custom_call" | custom-call | tf_op jit(solution)/shard_map/analysis/pallas_call | solution.py:632
  200.0 3.6 %hand_on.1 = f32[128,16,2,256]{3,2,1,0:T(2,128)} custom-call(f32[128,16,2,256]{3,2,1,0:T(2,128)} %get-tuple-element.6.source), custom_call_target="tpu_custom_call" | custom-call | tf_op jit(solution)/shard_map/hand_on/pallas_call | solution.py:647
